TPU v7x, 32 devices: a whole 2x2x4 slice. The times are simulated.
32 devices in a mesh: cfg: 2 (over core), tm: 16 (over z, y, x).
Axes of the slice: x: 2, y: 2, z: 4, core: 2. Of those that a mesh axis runs over, the one named last changes fastest.
Arguments:
- queries: bfloat16 [2, 12288, 1152], P('cfg', 'tm'), may hold values from -6 to 6
- key_vectors: bfloat16 [2, 12288, 1152], P('cfg', 'tm'), may hold values from -12 to 12
- value_vectors: bfloat16 [2, 12288, 1152], P('cfg', 'tm'), may hold values from -4 to 4
- out_weight: bfloat16 [1152, 2240], replicated, may hold values from -0.1875 to 0.1875
- first_frame: int32 [32], P('tm'), may hold values from 0 to 31, as said below
Outputs:
- guided: bfloat16 [12288, 2240], P('tm', 'cfg')
Inputs may be any that keep to these rules, and one draw needn't show every extreme that they name: first_frame[f] is 0 or lies between f - 4 and f; some frame f has first_frame[f] = f - 4.
All inputs are finite; a program needn't handle non-finite values.
Results may differ from a plain program's by a relative error of at most 0.014.
Values may be sent and summed in bfloat16 or wider, within the bound.
A program may use at most 192 MiB of HBM per device.

v0:
```python
import jax
import jax.numpy as jnp
from jax import lax
from jax.sharding import PartitionSpec as P

H = 36
DH = 32
FR = 2
NEAR = 2
FT = 384


guide_scale = 4.5
epsilon = 1e-06


def shifted(value, axis, steps):
    count = lax.axis_size(axis)
    initial, last = (max(0, -steps), min(count, count - steps))
    return lax.ppermute(value, axis, [(source, source + steps) for source in range(initial, last)])


def split_parts(values):
    upper = values.astype(jnp.bfloat16)
    lower = (values - upper.astype(jnp.float32)).astype(jnp.bfloat16)
    return jnp.concatenate([upper, lower], axis=-1)


def on_device(queries, key_vectors, value_vectors, out_weight, first_frame):
    rows_here = queries.shape[1]
    feature_width = queries.shape[2]
    query_frames = queries.reshape(FR, FT, H, DH)
    key_frames = jnp.maximum(key_vectors.reshape(FR, FT, H, DH), 0)
    value_frames = value_vectors.reshape(FR, FT, H, DH)
    frame_states = jnp.einsum(
        "fthd,fthe->fhde", key_frames, value_frames, preferred_element_type=jnp.float32
    )
    frame_sums = jnp.sum(key_frames, axis=1, dtype=jnp.float32)
    device_index = lax.axis_index("tm")
    local_ids = jnp.arange(FR, dtype=jnp.int32)
    own_frames = device_index * FR + local_ids
    source_states = [frame_states]
    source_sums = [frame_sums]
    source_frames = [own_frames]
    for offset in range(1, NEAR + 1):
        moved_states, moved_sums = (
            shifted(frame_states.astype(jnp.bfloat16), "tm", offset).astype(frame_states.dtype),
            shifted(frame_sums.astype(jnp.bfloat16), "tm", offset).astype(frame_sums.dtype),
        )
        source_states.append(moved_states)
        source_sums.append(moved_sums)
        source_frames.append((device_index - offset) * FR + local_ids)
    empty_states = jnp.zeros((H, DH, DH), jnp.float32)
    empty_sums = jnp.zeros((H, DH), jnp.float32)
    totals = (
        jnp.sum(frame_states, axis=0, keepdims=True),
        jnp.sum(frame_sums, axis=0, keepdims=True),
    )
    boundary = device_index - NEAR
    pieces = (
        lax.all_gather(totals[0].astype(jnp.bfloat16), "tm", axis=0, tiled=True).astype(
            jnp.float32
        ),
        lax.all_gather(totals[1].astype(jnp.bfloat16), "tm", axis=0, tiled=True).astype(
            jnp.float32
        ),
    )
    piece_count = pieces[0].shape[0]
    keeping = (jnp.arange(piece_count, dtype=jnp.int32) < boundary).astype(jnp.float32)
    added_states = jnp.einsum("n,nhde->hde", keeping, pieces[0], precision=lax.Precision.HIGHEST)
    added_sums = jnp.einsum("n,nhd->hd", keeping, pieces[1], precision=lax.Precision.HIGHEST)
    earlier_states = empty_states + added_states
    earlier_sums = empty_sums + added_sums
    all_states = jnp.concatenate(source_states + [earlier_states[None]], axis=0)
    all_sums = jnp.concatenate(source_sums + [earlier_sums[None]], axis=0)
    all_frames = jnp.concatenate(source_frames, axis=0)
    inside = (first_frame[:, None] <= all_frames[None, :]) & (
        all_frames[None, :] <= own_frames[:, None]
    )
    whole_prefix = (first_frame == 0)[:, None]
    mixing = jnp.concatenate([inside, whole_prefix], axis=1).astype(jnp.float32)
    attended_states = jnp.einsum(
        "is,shde->ihde", mixing, all_states, precision=lax.Precision.HIGHEST
    )
    attended_sums = jnp.einsum("is,shd->ihd", mixing, all_sums, precision=lax.Precision.HIGHEST)
    query_feats = jnp.maximum(query_frames, 0)
    state_parts = split_parts(attended_states)
    sum_parts = split_parts(attended_sums[..., None])
    numerator_parts = jnp.einsum(
        "ithd,ihde->ithe", query_feats, state_parts, preferred_element_type=jnp.float32
    )
    numerator = numerator_parts[..., :DH] + numerator_parts[..., DH:]
    denominator_parts = jnp.einsum(
        "ithd,ihde->ithe", query_feats, sum_parts, preferred_element_type=jnp.float32
    )
    denominator = denominator_parts[..., 0] + denominator_parts[..., 1] + epsilon
    attended = (
        (numerator / denominator[..., None]).astype(jnp.bfloat16).reshape(rows_here, feature_width)
    )
    projected = jnp.dot(attended, out_weight, preferred_element_type=jnp.float32)
    halves = lax.all_to_all(
        projected.astype(jnp.bfloat16), "cfg", split_axis=1, concat_axis=0, tiled=True
    ).astype(projected.dtype)
    cond_part = halves[:rows_here]
    uncond_part = halves[rows_here:]
    return (uncond_part + guide_scale * (cond_part - uncond_part)).astype(jnp.bfloat16)


def solution(mesh):
    placed = (P("cfg", "tm", None), P("cfg", "tm", None), P("cfg", "tm", None), P(), P("tm"))
    return jax.shard_map(
        on_device, mesh=mesh, in_specs=placed, out_specs=P("tm", "cfg"), check_vma=False
    )
```

profile of v0, /device:TPU:0, one launch (start us, length us, event | category | flops | bytes accessed | tf_op | source)
XLA Modules:
  0.0 162.6 jit_solution(10243039616867766528)
XLA Ops:
  6.5 2.6 %copy.51 = bf16[1,768,1152]{1,2,0:T(8,128)(2,1)S(1)} copy(bf16[1,768,1152]{2,1,0:T(8,128)(2,1)} %param.7) | data formatting | bytes 3538944 | tf_op args[2]
  9.2 1.9 %reshape.51 = bf16[2,384,36,32]{1,0,3,2:T(2,128)(2,1)} reshape(bf16[1,768,1152]{1,2,0:T(8,128)(2,1)S(1)} %copy.51) | data formatting | bytes 3538944 | tf_op jit(solution)/shard_map/reshape | solution.py:34
  11.1 0.5 fusion.41
  11.6 0.9 copy.50
  13.0 4.1 %fusion.42 = (bf16[36,32,32]{2,1,0:T(8,128)(2,1)}, f32[2,36,32,32]{3,2,1,0:T(8,128)}) fusion(bf16[2,384,36,32]{1,0,3,2:T(2,128)(2,1)} %reshape.51, bf16[2,384,36,32]{1,0,3,2:T(2,128)(2,1)S(1)} %max.18), kind=kOutput, calls=%fused_computation.64 | convolution fusion | flops 56659968 | bytes 3907584 | tf_op jit(solution)/shard_map/fthd,fthe->fhde/dot_general | solution.py:35
  17.1 2.0 %copy.55 = f32[2,36,32,32]{1,3,2,0:T(8,128)S(1)} copy(f32[2,36,32,32]{3,2,1,0:T(8,128)} %get-tuple-element.12) | data formatting | bytes 589824 | tf_op jit(solution)/shard_map/fthd,fthe->fhde/dot_general | solution.py:35
  19.1 0.9 convert_element_type.99
  20.0 5.8 %collective-permute-start.1 = (bf16[2,36,32,32]{1,3,2,0:T(8,128)(2,1)}, bf16[2,36,32,32]{1,3,2,0:T(8,128)(2,1)}, u32[]{:S(2)}, u32[]{:S(2)}) collective-permute-start(bf16[2,36,32,32]{1,3,2,0:T(8,128)(2,1)} %convert_element_type.99), channel_id=1, source_target_pairs={{0,2},{1,3},{2,4},{3,5},{4,6},{5,7},{6,8},{7,9},{8,10},{9,11},{10,... | collective-permute-start | bytes 442376 | tf_op jit(solution)/shard_map/ppermute | solution.py:20
  25.8 4.2 %collective-permute-start = (bf16[2,36,32,32]{1,3,2,0:T(8,128)(2,1)}, bf16[2,36,32,32]{1,3,2,0:T(8,128)(2,1)}, u32[]{:S(2)}, u32[]{:S(2)}) collective-permute-start(bf16[2,36,32,32]{1,3,2,0:T(8,128)(2,1)} %convert_element_type.99), channel_id=1, source_target_pairs={{0,1},{1,2},{2,3},{3,4},{4,5},{5,6},{6,7},{7,8},{8,9},{9,10},{10,1... | collective-permute-start | bytes 442376 | tf_op jit(solution)/shard_map/ppermute | solution.py:20
  30.0 1.5 convert_reduce_fusion
  31.9 1.9 %collective-permute-start.3 = (bf16[2,36,32]{1,0,2:T(2,128)(2,1)S(1)}, bf16[2,36,32]{1,0,2:T(2,128)(2,1)S(1)}, u32[]{:S(2)}, u32[]{:S(2)}) collective-permute-start(bf16[2,36,32]{1,0,2:T(2,128)(2,1)S(1)} %convert_element_type.108), channel_id=1, source_target_pairs={{0,2},{1,3},{2,4},{3,5},{4,6},{5,7},{6,8},{7,9},{8,10},{9,11},{10,... | collective-permute-start | bytes 13832 | tf_op jit(solution)/shard_map/ppermute | solution.py:20
  33.8 3.4 %collective-permute-start.2 = (bf16[2,36,32]{1,0,2:T(2,128)(2,1)S(1)}, bf16[2,36,32]{1,0,2:T(2,128)(2,1)S(1)}, u32[]{:S(2)}, u32[]{:S(2)}) collective-permute-start(bf16[2,36,32]{1,0,2:T(2,128)(2,1)S(1)} %convert_element_type.108), channel_id=1, source_target_pairs={{0,1},{1,2},{2,3},{3,4},{4,5},{5,6},{6,7},{7,8},{8,9},{9,10},{10,1... | collective-permute-start | bytes 13832 | tf_op jit(solution)/shard_map/ppermute | solution.py:20
  37.4 44.1 %all_gather.7 = bf16[16,36,32]{1,2,0:T(8,128)(2,1)S(1)} all-gather(bf16[1,36,32]{1,2,0:T(8,128)(2,1)S(1)} %copy.61), channel_id=1, replica_groups=mesh['cfg'=2,'tm'=16] {'tm'}, dimensions={0}, use_global_device_ids=true | all-gather | bytes 39168 | tf_op jit(solution)/shard_map/all_gather | solution.py:64
  81.8 1.6 %broadcast_maximum_fusion = bf16[1,768,1152]{2,1,0:T(8,128)(2,1)S(1)} fusion(bf16[1,768,1152]{2,1,0:T(8,128)(2,1)} %param.5), kind=kLoop, calls=%fused_computation.25 | loop fusion | flops 884736 | bytes 3538944 | tf_op jit(solution)/shard_map/max | solution.py:86
  83.6 2.3 %copy.57 = bf16[1,768,1152]{1,2,0:T(8,128)(2,1)} copy(bf16[1,768,1152]{2,1,0:T(8,128)(2,1)S(1)} %broadcast_maximum_fusion) | data formatting | bytes 3538944 | tf_op jit(solution)/shard_map/max | solution.py:86
  85.9 3.7 %max.20 = bf16[2,384,36,32]{1,0,3,2:T(2,128)(2,1)S(1)} reshape(bf16[1,768,1152]{1,2,0:T(8,128)(2,1)} %copy.57) | data formatting | bytes 3538944 | tf_op jit(solution)/shard_map/max | solution.py:86
  90.8 2.1 %convert_element_type.101 = f32[2,36,32,32]{1,3,2,0:T(8,128)} convert(bf16[2,36,32,32]{1,3,2,0:T(8,128)(2,1)} %collective-permute-done.1) | non-fusion elementwise | flops 73728 | bytes 442368 | tf_op jit(solution)/shard_map/convert_element_type | solution.py:47
  92.9 2.1 %convert_element_type.100 = f32[2,36,32,32]{1,3,2,0:T(8,128)} convert(bf16[2,36,32,32]{1,3,2,0:T(8,128)(2,1)} %collective-permute-done) | non-fusion elementwise | flops 73728 | bytes 442368 | tf_op jit(solution)/shard_map/convert_element_type | solution.py:47
  95.1 22.9 %all-gather.3.cloned.1.call-done = bf16[576,32,32]{2,1,0:T(8,128)(2,1)} async-done(((bf16[36,32,32]{2,1,0:T(8,128)(2,1)}), bf16[576,32,32]{2,1,0:T(8,128)(2,1)}) %all-gather.3.cloned.1.call-update) | async-done | bytes 1179664 | tf_op jit(solution)/shard_map/all_gather | solution.py:61
  117.9 8.8 %copy.69 = bf16[16,36,32,32]{1,0,3,2:T(8,128)(2,1)} copy(bf16[16,36,32,32]{3,2,1,0:T(8,128)(2,1)} %bitcast.75) | data formatting | bytes 2359296 | tf_op jit(solution)/shard_map/all_gather | solution.py:61
  126.7 3.0 %fusion.29 = f32[1,36,32,32]{1,0,3,2:T(1,128)S(1)} fusion(bf16[16,36,32,32]{1,0,3,2:T(8,128)(2,1)} %copy.69, s32[]{:T(128)S(6)} %sub.18), kind=kOutput, calls=%fused_computation.45 | convolution fusion | flops 1179664 | bytes 1327108 | tf_op jit(solution)/shard_map/n,nhde->hde/dot_general | solution.py:70
  129.7 0.7 pad_maximum_fusion
  130.4 4.5 %subtract_convert_fusion = (bf16[2,36,32,32]{1,0,3,2:T(2,128)(2,1)S(1)}, bf16[2,36,32,32]{1,0,3,2:T(2,128)(2,1)S(1)}) fusion(f32[7,36,32,32]{1,3,2,0:T(8,128)S(1)} %pad_maximum_fusion, pred[2,1]{1,0:T(4,128)(4,1)S(1)} %copy.49, pred[2,6]{1,0:T(4,128)(4,1)S(1)} %compare_and_fusion), kind=kOutput, calls=%fused_computation.24 | convolution fusion | flops 6488078 | bytes 1327118 | tf_op jit(solution)/shard_map/is,shde->ihde/dot_general | solution.py:82
  134.9 1.6 pad_maximum_fusion.1
  136.5 1.2 copy.58
  137.7 1.1 convolution_bitcast_fusion
  138.9 1.0 fusion.3
  139.9 1.8 %copy.67 = bf16[2,384,36,32]{1,0,3,2:T(2,128)(2,1)S(1)} copy(bf16[2,384,36,32]{1,3,2,0:T(8,128)(2,1)S(1)} %fusion.3) | data formatting | bytes 3538944 | tf_op jit(solution)/shard_map/convert_element_type | solution.py:98
  142.1 4.9 %convolution_convert_fusion = bf16[768,2240]{0,1:T(8,128)(2,1)S(1)} fusion(bf16[1152,2240]{0,1:T(8,128)(2,1)S(1)} %bitcast.81, bf16[768,1152]{0,1:T(8,128)(2,1)S(1)} %bitcast.78), kind=kOutput, calls=%fused_computation.1 | convolution fusion | flops 3965337600 | bytes 10371072 | tf_op jit(solution)/shard_map/dot_general | solution.py:100
  147.0 6.5 %all_to_all.13 = bf16[768,2,1120]{0,2,1:T(8,128)(2,1)S(1)} all-to-all(bf16[768,2,1120]{0,2,1:T(8,128)(2,1)S(1)} %bitcast.76), channel_id=1, replica_groups=mesh['cfg'=2,'tm'=16] {'cfg'}, dimensions={1} | all-to-all | bytes 6881280 | tf_op jit(solution)/shard_map/all_to_all | solution.py:101
  153.5 0.5 convert_bitcast_fusion
  154.0 1.7 %fusion.7 = bf16[768,1120]{0,1:T(8,128)(2,1)} fusion(f32[2,768,1120]{1,2,0:T(8,128)S(1)} %convert_bitcast_fusion), kind=kLoop, calls=%fused_computation.13 | loop fusion | flops 3440640 | bytes 8601600 | tf_op jit(solution)/shard_map/convert_element_type | solution.py:106
  (41 shorter events, 3.1 us)
Async XLA Ops:
  6.5 111.4 %all-gather.3.cloned.1.call-start = ((), (), s32[]{:S(2)}) async-start(), calls=%async_computation.1 | async-start | bytes 5013504 | tf_op jit(solution)/shard_map/all_gather | solution.py:61
  9.2 1.9 %copy-start.2 = (bf16[1,768,1152]{2,1,0:T(8,128)(2,1)S(1)}, bf16[1,768,1152]{2,1,0:T(8,128)(2,1)}, u32[]{:S(2)}) copy-start(bf16[1,768,1152]{2,1,0:T(8,128)(2,1)} %param.6) | copy-start | bytes 5308420
  20.0 61.6 %copy-start.3 = (s32[2]{0:T(128)S(1)}, s32[2]{0:T(128)}, u32[]{:S(2)}) copy-start(s32[2]{0:T(128)} %param.9) | copy-start | bytes 28
  20.0 70.8 %collective-permute-start.1 = (bf16[2,36,32,32]{1,3,2,0:T(8,128)(2,1)}, bf16[2,36,32,32]{1,3,2,0:T(8,128)(2,1)}, u32[]{:S(2)}, u32[]{:S(2)}) collective-permute-start(bf16[2,36,32,32]{1,3,2,0:T(8,128)(2,1)} %convert_element_type.99), channel_id=1, source_target_pairs={{0,2},{1,3},{2,4},{3,5},{4,6},{5,7},{6,8},{7,9},{8,10},{9,11},{10,... | collective-permute-start | bytes 442376 | tf_op jit(solution)/shard_map/ppermute | solution.py:20
  25.8 67.1 %collective-permute-start = (bf16[2,36,32,32]{1,3,2,0:T(8,128)(2,1)}, bf16[2,36,32,32]{1,3,2,0:T(8,128)(2,1)}, u32[]{:S(2)}, u32[]{:S(2)}) collective-permute-start(bf16[2,36,32,32]{1,3,2,0:T(8,128)(2,1)} %convert_element_type.99), channel_id=1, source_target_pairs={{0,1},{1,2},{2,3},{3,4},{4,5},{5,6},{6,7},{7,8},{8,9},{9,10},{10,1... | collective-permute-start | bytes 442376 | tf_op jit(solution)/shard_map/ppermute | solution.py:20
  31.9 57.7 %collective-permute-start.3 = (bf16[2,36,32]{1,0,2:T(2,128)(2,1)S(1)}, bf16[2,36,32]{1,0,2:T(2,128)(2,1)S(1)}, u32[]{:S(2)}, u32[]{:S(2)}) collective-permute-start(bf16[2,36,32]{1,0,2:T(2,128)(2,1)S(1)} %convert_element_type.108), channel_id=1, source_target_pairs={{0,2},{1,3},{2,4},{3,5},{4,6},{5,7},{6,8},{7,9},{8,10},{9,11},{10,... | collective-permute-start | bytes 13832 | tf_op jit(solution)/shard_map/ppermute | solution.py:20
  33.8 55.8 %collective-permute-start.2 = (bf16[2,36,32]{1,0,2:T(2,128)(2,1)S(1)}, bf16[2,36,32]{1,0,2:T(2,128)(2,1)S(1)}, u32[]{:S(2)}, u32[]{:S(2)}) collective-permute-start(bf16[2,36,32]{1,0,2:T(2,128)(2,1)S(1)} %convert_element_type.108), channel_id=1, source_target_pairs={{0,1},{1,2},{2,3},{3,4},{4,5},{5,6},{6,7},{7,8},{8,9},{9,10},{10,1... | collective-permute-start | bytes 13832 | tf_op jit(solution)/shard_map/ppermute | solution.py:20
  126.7 3.0 %copy-start = (f32[2,36,32,32]{1,3,2,0:T(8,128)S(1)}, f32[2,36,32,32]{1,3,2,0:T(8,128)}, u32[]{:S(2)}) copy-start(f32[2,36,32,32]{1,3,2,0:T(8,128)} %convert_element_type.101) | copy-start | bytes 884740
  126.7 3.0 %copy-start.1 = (f32[2,36,32,32]{1,3,2,0:T(8,128)S(1)}, f32[2,36,32,32]{1,3,2,0:T(8,128)}, u32[]{:S(2)}) copy-start(f32[2,36,32,32]{1,3,2,0:T(8,128)} %convert_element_type.100) | copy-start | bytes 884740
  137.7 4.4 %slice-start = ((s8[5160960]{0:T(1024)(128)(4,1)}), s8[4194304]{0:T(1024)(128)(4,1)S(1)}, s32[]{:S(2)}) async-start(s8[5160960]{0:T(1024)(128)(4,1)} %bitcast.80), calls=%async_computation.2 | async-start | bytes 8388608
  138.9 3.3 %slice-start.1 = ((s8[5160960]{0:T(1024)(128)(4,1)}), s8[966656]{0:T(1024)(128)(4,1)S(1)}, s32[]{:S(2)}) async-start(s8[5160960]{0:T(1024)(128)(4,1)} %bitcast.80), calls=%async_computation.3 | async-start | bytes 1933312
Sparse Core Ops, SparseCore 0:
  37.3 80.5 all-gather.2
where the time goes:
time: 163 us
  blocking collectives  50.6 us (31%)
  local copies, waits for them, and re-layouts  27 us (17%)
  waiting for transfers between devices  22.9 us (14%)
  matrix products  18.4 us (11%)
  starting transfers between devices  15.3 us (9%)
  other arithmetic  14.7 us (9%)
  between operations  13.7 us (8%)
    all_gather x1, blocking collectives, on_device(): lax.all_gather(totals[1].astype(jnp.bfloat16), 'tm', axis=0, tiled=True)  44.1 us
    all_gather x1, waiting for transfers between devices, on_device(): lax.all_gather(totals[0].astype(jnp.bfloat16), 'tm', axis=0, tiled=True)  22.9 us
    ppermute x4, starting transfers between devices, shifted(): lax.ppermute(value, axis, [(source, source + steps) for source in range(i...  15.3 us
    all_gather x1, local copies, waits for them, and re-layouts, on_device(): lax.all_gather(totals[0].astype(jnp.bfloat16), 'tm', axis=0, tiled=True)  8.76 us
    all_to_all x1, blocking collectives, on_device(): lax.all_to_all(projected.astype(jnp.bfloat16), 'cfg', split_axis=1, conca...  6.48 us
    max x2, local copies, waits for them, and re-layouts, on_device(): query_feats = jnp.maximum(query_frames, 0)  5.94 us
    dot_general x1, matrix products, on_device(): jnp.dot(attended, out_weight, preferred_element_type=jnp.float32)  4.87 us
    dot_general x1, matrix products, on_device(): jnp.einsum('is,shde->ihde', mixing, all_states, precision=lax.Precision.H...  4.47 us
  transfers between devices with their start and end apart: 5, of which 1 were waited for; matrix products, arithmetic and copies ran while one was open for 10% of the time, Pallas kernels for 0%

commit v1 on v0

v1 whole, which is shorter than its diff:
```python
import functools

import jax
import jax.numpy as jnp
from jax import lax
from jax.experimental import pallas as pl
from jax.experimental.pallas import tpu as pltpu
from jax.sharding import PartitionSpec as P

DH = 32
NEAR = 2
LANES = 128
PER = LANES // DH

guide_scale = 4.5
epsilon = 1e-06


def head_mask(rows, block):
    row = lax.broadcasted_iota(jnp.int32, (rows, LANES), 0) // DH
    lane = lax.broadcasted_iota(jnp.int32, (rows, LANES), 1) // DH
    return lane == (block if rows == DH else row)


def states_kernel(
    n, bits, ff_ref, q_ref, k_ref, v_ref, st_ref, qo_ref,
    kbuf, vbuf, frames, near_out, near_in, tot, pre, tot_out, tot_in, fin, other,
    load_sem, tot_send, tot_recv, near_send, near_recv, q_sem, fin_sem,
):
    fr = frames.shape[0]
    ft = kbuf.shape[0] // fr
    groups = kbuf.shape[1] // LANES
    base = groups * DH
    me = lax.axis_index("tm")
    other_core = 1 - lax.axis_index("cfg")

    loads = []
    for f in range(fr):
        rows = pl.ds(f * ft, ft)
        for which, (src, dst) in enumerate(((k_ref, kbuf), (v_ref, vbuf))):
            copy = pltpu.make_async_copy(src.at[rows], dst.at[rows], load_sem.at[2 * f + which])
            copy.start()
            loads.append(copy)

    def partner(k):
        bit = (me // (1 << k)) % 2
        return bit, me + (1 - 2 * bit) * (1 << k)

    barrier = pltpu.get_barrier_semaphore()
    pl.semaphore_signal(barrier, inc=1, device_id={"cfg": other_core})
    count = jnp.int32(1 + bits)
    for k in range(bits):
        pl.semaphore_signal(barrier, inc=1, device_id={"tm": partner(k)[1]})
    for d in range(1, NEAR + 1):
        @pl.when(me + d < n)
        def _():
            pl.semaphore_signal(barrier, inc=1, device_id={"tm": me + d})

        @pl.when(me >= d)
        def _():
            pl.semaphore_signal(barrier, inc=1, device_id={"tm": me - d})

        count = count + jnp.where(me + d < n, 1, 0) + jnp.where(me >= d, 1, 0)

    masks = [head_mask(DH, a) for a in range(PER)]
    for f in range(fr):
        loads[2 * f].wait()
        loads[2 * f + 1].wait()
        frames[f, base:, :] = jnp.zeros((frames.shape[1] - base, LANES), jnp.float32)
        for g in range(groups):
            cols = slice(g * LANES, (g + 1) * LANES)
            keys = jnp.maximum(kbuf[f * ft:(f + 1) * ft, cols], 0)
            values = vbuf[f * ft:(f + 1) * ft, cols]
            full = lax.dot_general(
                values, keys, (((0,), (0,)), ((), ())), preferred_element_type=jnp.float32
            )
            compact = jnp.zeros((DH, LANES), jnp.float32)
            for a in range(PER):
                compact = jnp.where(masks[a], full[a * DH:(a + 1) * DH], compact)
            frames[f, g * DH:(g + 1) * DH, :] = compact
            frames[f, base + g:base + g + 1, :] = jnp.sum(
                keys.astype(jnp.float32), axis=0, keepdims=True
            )
    near_out[...] = frames[...].astype(jnp.bfloat16)
    total = frames[0]
    for f in range(1, fr):
        total = total + frames[f]
    tot[...] = total
    tot_out[0] = total.astype(jnp.bfloat16)
    pre[...] = jnp.zeros_like(pre)
    for d in range(1, NEAR + 1):
        @pl.when(me < d)
        def _():
            near_in[d - 1] = jnp.zeros(near_in.shape[1:], jnp.bfloat16)

    pl.semaphore_wait(barrier, count)

    def near_copy(d):
        return pltpu.make_async_remote_copy(
            src_ref=near_out, dst_ref=near_in.at[d - 1], send_sem=near_send.at[d - 1],
            recv_sem=near_recv.at[d - 1], device_id={"tm": me + d},
        )

    def start_near(d):
        @pl.when(me + d < n)
        def _():
            near_copy(d).start()

    q_copy = pltpu.make_async_remote_copy(
        src_ref=q_ref, dst_ref=qo_ref, send_sem=q_sem.at[0], recv_sem=q_sem.at[1],
        device_id={"cfg": other_core},
    )
    for k in range(bits):
        bit, peer = partner(k)
        copy = pltpu.make_async_remote_copy(
            src_ref=tot_out.at[k], dst_ref=tot_in.at[k], send_sem=tot_send.at[k],
            recv_sem=tot_recv.at[k], device_id={"tm": peer},
        )
        if k < bits - 1:
            copy.start()
            if k == 0:
                start_near(2)
                q_copy.start()
            if k == min(1, bits - 2):
                start_near(1)
            copy.wait_recv()
            got = tot_in[k].astype(jnp.float32)
            pre[...] += jnp.where(bit == 1, 1.0, 0.0) * got
            tot[...] += got
            tot_out[k + 1] = tot[...].astype(jnp.bfloat16)
            copy.wait_send()
        else:
            @pl.when(bit == 0)
            def _():
                copy.start()
                copy.wait_send()

            @pl.when(bit == 1)
            def _():
                copy.wait_recv()
                pre[...] += tot_in[k].astype(jnp.float32)

    for d in range(1, NEAR + 1):
        @pl.when(me >= d)
        def _():
            near_copy(d).wait_recv()

        @pl.when(me + d < n)
        def _():
            near_copy(d).wait_send()

    for j in range(fr):
        first = ff_ref[j]
        whole = first == 0
        acc = jnp.where(whole, 1.0, 0.0) * pre[...]
        for f in range(j + 1):
            acc = acc + jnp.where(me * fr + f >= first, 1.0, 0.0) * frames[f]
        for d in range(1, NEAR + 1):
            for f in range(fr):
                inside = jnp.logical_and(first > 0, (me - d) * fr + f >= first)
                acc = acc + jnp.where(inside, 1.0, 0.0) * near_in[d - 1, f].astype(jnp.float32)
        fin[j] = acc
        st_ref[0, j] = acc
    fin_copy = pltpu.make_async_remote_copy(
        src_ref=fin, dst_ref=other, send_sem=fin_sem.at[0], recv_sem=fin_sem.at[1],
        device_id={"cfg": other_core},
    )
    fin_copy.start()
    fin_copy.wait()
    st_ref[1] = other[...]
    q_copy.wait()


def project_kernel(per_frame, st_ref, q_ref, qo_ref, w_ref, o_ref, mats, comb):
    groups = q_ref.shape[1] // LANES
    base = groups * DH
    core = lax.axis_index("cfg")
    own_scale = jnp.where(core == 0, guide_scale, 1.0 - guide_scale)
    other_scale = jnp.where(core == 0, 1.0 - guide_scale, guide_scale)

    @pl.when(pl.program_id(0) % per_frame == 0)
    def _():
        frame = pl.program_id(0) // per_frame
        diagonal = head_mask(LANES, 0)
        for b in range(2):
            for g in range(groups):
                compact = st_ref[b, frame, g * DH:(g + 1) * DH, :]
                sums = st_ref[b, frame, base + g:base + g + 1, :]
                state = jnp.where(diagonal, jnp.concatenate([compact] * PER, axis=0), 0.0)
                total = jnp.where(diagonal, jnp.broadcast_to(sums, (LANES, LANES)), 0.0)
                both = jnp.concatenate([state, total], axis=0)
                upper = both.astype(jnp.bfloat16)
                lower = (both - upper.astype(jnp.float32)).astype(jnp.bfloat16)
                mats[b, g] = jnp.concatenate([upper, lower], axis=1)

    for g in range(groups):
        cols = slice(g * LANES, (g + 1) * LANES)
        parts = []
        for b, ref in enumerate((q_ref, qo_ref)):
            feats = jnp.maximum(ref[:, cols], 0)
            both = lax.dot_general(
                jnp.concatenate([feats, feats], axis=1), mats[b, g],
                (((1,), (1,)), ((), ())), preferred_element_type=jnp.float32,
            )
            parts.append((both[:, :LANES], both[:, LANES:] + epsilon))
        (own, own_den), (oth, oth_den) = parts
        mixed = (own_scale * own * oth_den + other_scale * oth * own_den) / (own_den * oth_den)
        comb[:, cols] = mixed.astype(jnp.bfloat16)
    o_ref[...] = jnp.dot(
        comb[...], w_ref[...], preferred_element_type=jnp.float32
    ).astype(o_ref.dtype)


def on_device(n, cores, queries, key_vectors, value_vectors, out_weight, first_frame):
    rows, width = queries.shape[1:]
    fr = first_frame.shape[0]
    bits = n.bit_length() - 1
    groups = width // LANES
    height = groups * DH + 16 * pl.cdiv(groups, 16)
    block = (height, LANES)
    flat = lambda a: a.reshape(rows, width)
    queries = flat(queries)
    f32, bf16 = jnp.float32, jnp.bfloat16
    hbm = pl.BlockSpec(memory_space=pl.ANY)
    vmem = pl.BlockSpec(memory_space=pltpu.VMEM)
    states, other_queries = pl.pallas_call(
        functools.partial(states_kernel, n, bits),
        name="states",
        out_shape=(
            jax.ShapeDtypeStruct((2, fr) + block, f32),
            jax.ShapeDtypeStruct((rows, width), bf16),
        ),
        in_specs=[pl.BlockSpec(memory_space=pltpu.SMEM), hbm, hbm, hbm],
        out_specs=(vmem, hbm),
        scratch_shapes=[
            pltpu.VMEM((rows, width), bf16),
            pltpu.VMEM((rows, width), bf16),
            pltpu.VMEM((fr,) + block, f32),
            pltpu.VMEM((fr,) + block, bf16),
            pltpu.VMEM((NEAR, fr) + block, bf16),
            pltpu.VMEM(block, f32),
            pltpu.VMEM(block, f32),
            pltpu.VMEM((bits,) + block, bf16),
            pltpu.VMEM((bits,) + block, bf16),
            pltpu.VMEM((fr,) + block, f32),
            pltpu.VMEM((fr,) + block, f32),
            pltpu.SemaphoreType.DMA((2 * fr,)),
            pltpu.SemaphoreType.DMA((bits,)),
            pltpu.SemaphoreType.DMA((bits,)),
            pltpu.SemaphoreType.DMA((NEAR,)),
            pltpu.SemaphoreType.DMA((NEAR,)),
            pltpu.SemaphoreType.DMA((2,)),
            pltpu.SemaphoreType.DMA((2,)),
        ],
        compiler_params=pltpu.CompilerParams(
            collective_id=0, has_side_effects=True, vmem_limit_bytes=24 << 20
        ),
    )(first_frame, queries, flat(key_vectors), flat(value_vectors))

    columns = out_weight.shape[1] // cores
    weight = lax.dynamic_slice_in_dim(
        out_weight, lax.axis_index("cfg") * columns, columns, axis=1
    )
    per_frame = 2
    tile = rows // (fr * per_frame)
    return pl.pallas_call(
        functools.partial(project_kernel, per_frame),
        name="project",
        grid=(fr * per_frame,),
        out_shape=jax.ShapeDtypeStruct((rows, columns), bf16),
        in_specs=[
            pl.BlockSpec((2, fr) + block, lambda i: (0, 0, 0, 0)),
            pl.BlockSpec((tile, width), lambda i: (i, 0)),
            pl.BlockSpec((tile, width), lambda i: (i, 0)),
            pl.BlockSpec((width, columns), lambda i: (0, 0)),
        ],
        out_specs=pl.BlockSpec((tile, columns), lambda i: (i, 0)),
        scratch_shapes=[
            pltpu.VMEM((2, groups, 2 * LANES, 2 * LANES), bf16),
            pltpu.VMEM((tile, width), bf16),
        ],
        compiler_params=pltpu.CompilerParams(
            dimension_semantics=("arbitrary",), vmem_limit_bytes=32 << 20
        ),
    )(states, queries, other_queries, weight)


def solution(mesh):
    placed = (P("cfg", "tm", None), P("cfg", "tm", None), P("cfg", "tm", None), P(), P("tm"))
    return jax.shard_map(
        functools.partial(on_device, mesh.shape["tm"], mesh.shape["cfg"]),
        mesh=mesh, in_specs=placed, out_specs=P("tm", "cfg"), check_vma=False,
    )
```

time: 163 us -> 47.3 us (0.29)
  blocking collectives: 50.6 us -> 0 us
  Pallas kernels: 0 us -> 29.9 us
  waiting for transfers between devices: 22.9 us -> 0 us
  matrix products: 18.4 us -> 0 us
  starting transfers between devices: 15.3 us -> 0 us
  other arithmetic: 14.7 us -> 0 us
  between operations: 13.7 us -> 0.06 us
  local copies, waits for them, and re-layouts: 27 us -> 17 us
    all_gather x1 -> x0, blocking collectives: 44.1 us -> none  [on_device(): lax.all_gather(totals[1].astype(jnp.bfloat16), 'tm', axis=0, tiled=True)]
    pallas_call x0 -> x2, Pallas kernels: none -> 29.9 us  [the longest x1 22.8 us: on_device(): pl.pallas_call(functools.partial(states_kernel, n, bits), name='states',...]
    all_gather x1 -> x0, waiting for transfers between devices: 22.9 us -> none  [on_device(): lax.all_gather(totals[0].astype(jnp.bfloat16), 'tm', axis=0, tiled=True)]
    dot_general x8 -> x0, matrix products: 18.4 us -> none  [the longest x1 4.87 us: on_device(): jnp.dot(attended, out_weight, preferred_element_type=jnp.float32)]
    ppermute x4 -> x0, starting transfers between devices: 15.3 us -> none  [shifted(): lax.ppermute(value, axis, [(source, source + steps) for source in range(i...]
    all_gather x1 -> x0, local copies, waits for them, and re-layouts: 8.76 us -> none  [on_device(): lax.all_gather(totals[0].astype(jnp.bfloat16), 'tm', axis=0, tiled=True)]
    convert_element_type x9 -> x0, other arithmetic: 8.48 us -> none  [the longest x2 4.29 us: on_device(): shifted(frame_states.astype(jnp.bfloat16), 'tm', offset)]
    max x4 -> x0, local copies, waits for them, and re-layouts: 7.33 us -> none  [the longest x2 5.94 us: on_device(): query_feats = jnp.maximum(query_frames, 0)]
  transfers between devices with their start and end apart: 5 -> 0, of which waited for: 1 -> 0; matrix products, arithmetic and copies ran while one was open for 10% -> 0% of each run, Pallas kernels for 0% -> 0%
where the time goes in v1:
time: 47.3 us; the launch traced here: 46.9 us
  Pallas kernels  29.9 us (63%)
  local copies, waits for them, and re-layouts  17 us (36%)
    pallas_call x1, Pallas kernels, on_device(): pl.pallas_call(functools.partial(states_kernel, n, bits), name='states',...  22.8 us
    unnamed x13, local copies, waits for them, and re-layouts  9.76 us
    pallas_call x1, Pallas kernels, on_device(): pl.pallas_call(functools.partial(project_kernel, per_frame), name='projec...  7.04 us
    pallas_call x1, local copies, waits for them, and re-layouts, on_device(): pl.pallas_call(functools.partial(project_kernel, per_frame), name='projec...  3.81 us
    dynamic_slice x1, local copies, waits for them, and re-layouts, on_device(): lax.dynamic_slice_in_dim(out_weight, lax.axis_index('cfg') * columns, col...  3.41 us

profile of v1, /device:TPU:0, one launch (start us, length us, event | category | flops | bytes accessed | tf_op | source)
XLA Modules:
  0.0 46.9 jit_solution(3257768267142979015)
XLA Ops:
  0.0 3.4 %constant_dynamic-slice_fusion = bf16[1152,1120]{0,1:T(8,128)(2,1)} fusion(bf16[1152,2240]{0,1:T(8,128)(2,1)} %param.8, s32[]{:T(128)S(6)} %select_n.3), kind=kLoop, calls=%fused_computation | loop fusion | bytes 5160964 | tf_op jit(solution)/shard_map/dynamic_slice | solution.py:261
  3.4 0.0 copy-start.5
  3.4 4.1 %copy.8.w_ref = bf16[1152,1120]{1,0:T(8,128)(2,1)S(1)} copy(bf16[1152,1120]{0,1:T(8,128)(2,1)} %constant_dynamic-slice_fusion) | data formatting | bytes 5160960
  7.5 0.0 copy-done.5
  7.5 0.0 copy-start
  7.5 1.5 %copy-done = bf16[1,768,1152]{2,1,0:T(8,128)(2,1)S(1)} copy-done((bf16[1,768,1152]{2,1,0:T(8,128)(2,1)S(1)}, bf16[1,768,1152]{2,1,0:T(8,128)(2,1)}, u32[]{:S(2)}) %copy-start) | copy-done | bytes 1769496
  9.0 0.0 copy-start.3
  9.0 1.5 %copy-done.3 = bf16[1,768,1152]{2,1,0:T(8,128)(2,1)S(1)} copy-done((bf16[1,768,1152]{2,1,0:T(8,128)(2,1)S(1)}, bf16[1,768,1152]{2,1,0:T(8,128)(2,1)}, u32[]{:S(2)}) %copy-start.3) | copy-done | bytes 1769496
  10.5 0.0 copy-start.4
  10.5 1.5 %copy-done.4 = bf16[1,768,1152]{2,1,0:T(8,128)(2,1)S(1)} copy-done((bf16[1,768,1152]{2,1,0:T(8,128)(2,1)S(1)}, bf16[1,768,1152]{2,1,0:T(8,128)(2,1)}, u32[]{:S(2)}) %copy-start.4) | copy-done | bytes 1769496
  12.0 0.0 copy-start.1
  12.0 22.8 %states.1 = (f32[2,2,304,128]{3,2,1,0:T(8,128)S(1)}, bf16[768,1152]{1,0:T(8,128)(2,1)S(1)}) custom-call(s32[2]{0:T(128)S(1)} %copy-done.5, bf16[768,1152]{1,0:T(8,128)(2,1)S(1)} %bitcast.3, bf16[768,1152]{1,0:T(8,128)(2,1)S(1)} %bitcast.5, bf16[768,1152]{1,0:T(8,128)(2,1)S(1)} %bitcast.6), custom_call_target="tpu_custom_call" | custom-call | tf_op jit(solution)/shard_map/states/pallas_call | solution.py:226
  34.8 0.0 copy-done.1
  34.8 7.0 %project.1 = bf16[768,1120]{1,0:T(8,128)(2,1)S(1)} custom-call(f32[2,2,304,128]{3,2,1,0:T(8,128)S(1)} %get-tuple-element.7.st_ref, bf16[768,1152]{1,0:T(8,128)(2,1)S(1)} %bitcast.4, bf16[768,1152]{1,0:T(8,128)(2,1)S(1)} %get-tuple-element.8.qo_ref, bf16[1152,1120]{1,0:T(8,128)(2,1)S(1)} %copy.8.w_ref), custom_call_target="tpu_custom_call" | custom-call | tf_op jit(solution)/shard_map/project/pallas_call | solution.py:266
  41.9 0.0 copy-start.2
  41.9 1.2 %copy-done.2 = bf16[768,1120]{1,0:T(8,128)(2,1)} copy-done((bf16[768,1120]{1,0:T(8,128)(2,1)}, bf16[768,1120]{1,0:T(8,128)(2,1)S(1)}, u32[]{:S(2)}) %copy-start.2) | copy-done | bytes 1720344
  43.1 3.8 %copy.7 = bf16[768,1120]{0,1:T(8,128)(2,1)} copy(bf16[768,1120]{1,0:T(8,128)(2,1)} %copy-done.2) | data formatting | bytes 3440640 | tf_op jit(solution)/shard_map/project/pallas_call | solution.py:266
Async XLA Ops:
  3.4 4.1 %copy-start.5 = (s32[2]{0:T(128)S(1)}, s32[2]{0:T(128)}, u32[]{:S(2)}) copy-start(s32[2]{0:T(128)} %ff_ref.1) | copy-start | bytes 28
  7.5 1.5 %copy-start = (bf16[1,768,1152]{2,1,0:T(8,128)(2,1)S(1)}, bf16[1,768,1152]{2,1,0:T(8,128)(2,1)}, u32[]{:S(2)}) copy-start(bf16[1,768,1152]{2,1,0:T(8,128)(2,1)} %param.5) | copy-start | bytes 5308420
  9.0 1.5 %copy-start.3 = (bf16[1,768,1152]{2,1,0:T(8,128)(2,1)S(1)}, bf16[1,768,1152]{2,1,0:T(8,128)(2,1)}, u32[]{:S(2)}) copy-start(bf16[1,768,1152]{2,1,0:T(8,128)(2,1)} %param.6) | copy-start | bytes 5308420
  10.5 1.5 %copy-start.4 = (bf16[1,768,1152]{2,1,0:T(8,128)(2,1)S(1)}, bf16[1,768,1152]{2,1,0:T(8,128)(2,1)}, u32[]{:S(2)}) copy-start(bf16[1,768,1152]{2,1,0:T(8,128)(2,1)} %param.7) | copy-start | bytes 5308420
  12.0 22.8 %copy-start.1 = (bf16[1,768,1152]{2,1,0:T(8,128)(2,1)S(1)}, bf16[1,768,1152]{2,1,0:T(8,128)(2,1)}, u32[]{:S(2)}) copy-start(bf16[1,768,1152]{2,1,0:T(8,128)(2,1)} %param.5) | copy-start | bytes 5308420
  41.9 1.2 %copy-start.2 = (bf16[768,1120]{1,0:T(8,128)(2,1)}, bf16[768,1120]{1,0:T(8,128)(2,1)S(1)}, u32[]{:S(2)}) copy-start(bf16[768,1120]{1,0:T(8,128)(2,1)S(1)} %project.1) | copy-start | bytes 5160964

commit v2 on v1

--- a/solution.py
+++ b/solution.py
@@ -171,44 +171,69 @@
     q_copy.wait()
 
 
-def project_kernel(per_frame, st_ref, q_ref, qo_ref, w_ref, o_ref, mats, comb):
+def project_kernel(st_ref, q_ref, qo_ref, w_ref, o_ref, qbuf, wbuf, comb, obuf, load_sem, out_sem):
+    fr = st_ref.shape[1]
+    columns = wbuf.shape[0]
     groups = q_ref.shape[1] // LANES
     base = groups * DH
+    ft = comb.shape[0] // fr
+    tile = ft if ft % 256 == 0 else 2 * LANES
     core = lax.axis_index("cfg")
+    q_copies = [
+        pltpu.make_async_copy(src, qbuf.at[b], load_sem.at[1 + b])
+        for b, src in enumerate((q_ref, qo_ref))
+    ]
+    for copy in q_copies:
+        copy.start()
+    w_copy = pltpu.make_async_copy(
+        w_ref.at[pl.ds(pl.multiple_of(core * columns, 16), columns)], wbuf, load_sem.at[0]
+    )
+    w_copy.start()
     own_scale = jnp.where(core == 0, guide_scale, 1.0 - guide_scale)
     other_scale = jnp.where(core == 0, 1.0 - guide_scale, guide_scale)
-
-    @pl.when(pl.program_id(0) % per_frame == 0)
-    def _():
-        frame = pl.program_id(0) // per_frame
-        diagonal = head_mask(LANES, 0)
-        for b in range(2):
-            for g in range(groups):
-                compact = st_ref[b, frame, g * DH:(g + 1) * DH, :]
-                sums = st_ref[b, frame, base + g:base + g + 1, :]
-                state = jnp.where(diagonal, jnp.concatenate([compact] * PER, axis=0), 0.0)
-                total = jnp.where(diagonal, jnp.broadcast_to(sums, (LANES, LANES)), 0.0)
-                both = jnp.concatenate([state, total], axis=0)
-                upper = both.astype(jnp.bfloat16)
-                lower = (both - upper.astype(jnp.float32)).astype(jnp.bfloat16)
-                mats[b, g] = jnp.concatenate([upper, lower], axis=1)
-
-    for g in range(groups):
-        cols = slice(g * LANES, (g + 1) * LANES)
-        parts = []
-        for b, ref in enumerate((q_ref, qo_ref)):
-            feats = jnp.maximum(ref[:, cols], 0)
-            both = lax.dot_general(
-                jnp.concatenate([feats, feats], axis=1), mats[b, g],
-                (((1,), (1,)), ((), ())), preferred_element_type=jnp.float32,
-            )
-            parts.append((both[:, :LANES], both[:, LANES:] + epsilon))
-        (own, own_den), (oth, oth_den) = parts
-        mixed = (own_scale * own * oth_den + other_scale * oth * own_den) / (own_den * oth_den)
-        comb[:, cols] = mixed.astype(jnp.bfloat16)
-    o_ref[...] = jnp.dot(
-        comb[...], w_ref[...], preferred_element_type=jnp.float32
-    ).astype(o_ref.dtype)
+    diagonal = head_mask(LANES, 0)
+
+    def matrices(b, frame, g):
+        compact = st_ref[b, frame, g * DH:(g + 1) * DH, :]
+        sums = st_ref[b, frame, base + g:base + g + 1, :]
+        state = jnp.where(diagonal, jnp.concatenate([compact] * PER, axis=0), 0.0)
+        total = jnp.where(diagonal, jnp.broadcast_to(sums, (LANES, LANES)), 0.0)
+        both = jnp.concatenate([state, total], axis=0)
+        upper = both.astype(jnp.bfloat16)
+        lower = (both - upper.astype(jnp.float32)).astype(jnp.bfloat16)
+        return jnp.concatenate([upper, lower], axis=1)
+
+    for copy in q_copies:
+        copy.wait()
+    for f in range(fr):
+        rows = slice(f * ft, (f + 1) * ft)
+        for g in range(groups):
+            cols = slice(g * LANES, (g + 1) * LANES)
+            parts = []
+            for b in range(2):
+                feats = jnp.maximum(qbuf[b, rows, cols], 0)
+                both = lax.dot_general(
+                    jnp.concatenate([feats, feats], axis=1), matrices(b, f, g),
+                    (((1,), (1,)), ((), ())), preferred_element_type=jnp.float32,
+                )
+                parts.append((both[:, :LANES], both[:, LANES:] + epsilon))
+            (own, own_den), (oth, oth_den) = parts
+            mixed = (own_scale * own * oth_den + other_scale * oth * own_den) / (own_den * oth_den)
+            comb[rows, cols] = mixed.astype(jnp.bfloat16)
+    w_copy.wait()
+    outs = []
+    for t in range(comb.shape[0] // tile):
+        part = slice(t * tile, (t + 1) * tile)
+        obuf[:, part] = lax.dot_general(
+            wbuf[...], comb[part, :], (((1,), (1,)), ((), ())),
+            preferred_element_type=jnp.float32,
+        ).astype(obuf.dtype)
+        span = pl.ds(t * tile, tile)
+        copy = pltpu.make_async_copy(obuf.at[:, span], o_ref.at[:, span], out_sem.at[t])
+        copy.start()
+        outs.append(copy)
+    for copy in outs:
+        copy.wait()
 
 
 def on_device(n, cores, queries, key_vectors, value_vectors, out_weight, first_frame):
@@ -221,7 +246,7 @@
     flat = lambda a: a.reshape(rows, width)
     queries = flat(queries)
     f32, bf16 = jnp.float32, jnp.bfloat16
-    hbm = pl.BlockSpec(memory_space=pl.ANY)
+    hbm = pl.BlockSpec(memory_space=pltpu.HBM)
     vmem = pl.BlockSpec(memory_space=pltpu.VMEM)
     states, other_queries = pl.pallas_call(
         functools.partial(states_kernel, n, bits),
@@ -253,36 +278,27 @@
             pltpu.SemaphoreType.DMA((2,)),
         ],
         compiler_params=pltpu.CompilerParams(
-            collective_id=0, has_side_effects=True, vmem_limit_bytes=24 << 20
+            collective_id=0, has_side_effects=True
         ),
     )(first_frame, queries, flat(key_vectors), flat(value_vectors))
 
     columns = out_weight.shape[1] // cores
-    weight = lax.dynamic_slice_in_dim(
-        out_weight, lax.axis_index("cfg") * columns, columns, axis=1
-    )
-    per_frame = 2
-    tile = rows // (fr * per_frame)
-    return pl.pallas_call(
-        functools.partial(project_kernel, per_frame),
+    flipped = pl.pallas_call(
+        project_kernel,
         name="project",
-        grid=(fr * per_frame,),
-        out_shape=jax.ShapeDtypeStruct((rows, columns), bf16),
-        in_specs=[
-            pl.BlockSpec((2, fr) + block, lambda i: (0, 0, 0, 0)),
-            pl.BlockSpec((tile, width), lambda i: (i, 0)),
-            pl.BlockSpec((tile, width), lambda i: (i, 0)),
-            pl.BlockSpec((width, columns), lambda i: (0, 0)),
+        out_shape=jax.ShapeDtypeStruct((columns, rows), bf16),
+        in_specs=[vmem, hbm, hbm, hbm],
+        out_specs=hbm,
+        scratch_shapes=[
+            pltpu.VMEM((2, rows, width), bf16),
+            pltpu.VMEM((columns, width), bf16),
+            pltpu.VMEM((rows, width), bf16),
+            pltpu.VMEM((columns, rows), bf16),
+            pltpu.SemaphoreType.DMA((3,)),
+            pltpu.SemaphoreType.DMA((rows // LANES,)),
         ],
-        out_specs=pl.BlockSpec((tile, columns), lambda i: (i, 0)),
-        scratch_shapes=[
-            pltpu.VMEM((2, groups, 2 * LANES, 2 * LANES), bf16),
-            pltpu.VMEM((tile, width), bf16),
-        ],
-        compiler_params=pltpu.CompilerParams(
-            dimension_semantics=("arbitrary",), vmem_limit_bytes=32 << 20
-        ),
-    )(states, queries, other_queries, weight)
+            )(states, queries, other_queries, out_weight.T)
+    return flipped.T
 
 
 def solution(mesh):

time: 47.3 us -> 32.4 us (0.68)
  local copies, waits for them, and re-layouts: 17 us -> 0 us
  Pallas kernels: 29.9 us -> 32.2 us
    unnamed x13 -> x0, local copies, waits for them, and re-layouts: 9.76 us -> none
    pallas_call x1 -> x0, local copies, waits for them, and re-layouts: 3.81 us -> none  [on_device(): pl.pallas_call(functools.partial(project_kernel, per_frame), name='projec...]
    dynamic_slice x1 -> x0, local copies, waits for them, and re-layouts: 3.41 us -> none  [on_device(): lax.dynamic_slice_in_dim(out_weight, lax.axis_index('cfg') * columns, col...]
    pallas_call x1, Pallas kernels: 7.04 us -> 9.03 us  [on_device(): pl.pallas_call(project_kernel, name='project', out_shape=jax.ShapeDtypeSt...]
where the time goes in v2:
time: 32.4 us; the launch traced here: 32.2 us
  Pallas kernels  32.2 us (99%)
    pallas_call x1, Pallas kernels, on_device(): pl.pallas_call(functools.partial(states_kernel, n, bits), name='states',...  23.2 us
    pallas_call x1, Pallas kernels, on_device(): pl.pallas_call(project_kernel, name='project', out_shape=jax.ShapeDtypeSt...  9.03 us

profile of v2, /device:TPU:0, one launch (start us, length us, event | category | flops | bytes accessed | tf_op | source)
XLA Modules:
  0.0 32.2 jit_solution(2462554087786313130)
XLA Ops:
  0.0 23.2 %states.1 = (f32[2,2,304,128]{3,2,1,0:T(8,128)}, bf16[768,1152]{1,0:T(8,128)(2,1)}) custom-call(s32[2]{0:T(128)} %ff_ref.1, bf16[768,1152]{1,0:T(8,128)(2,1)} %bitcast.5, bf16[768,1152]{1,0:T(8,128)(2,1)} %bitcast.8, bf16[768,1152]{1,0:T(8,128)(2,1)} %bitcast.9), custom_call_target="tpu_custom_call" | custom-call | tf_op jit(solution)/shard_map/states/pallas_call | solution.py:251
  23.2 9.0 %project.1 = bf16[1120,768]{1,0:T(8,128)(2,1)} custom-call(f32[2,2,304,128]{3,2,1,0:T(8,128)} %get-tuple-element.7.st_ref, bf16[768,1152]{1,0:T(8,128)(2,1)} %bitcast.6, bf16[768,1152]{1,0:T(8,128)(2,1)} %get-tuple-element.8.qo_ref, bf16[2240,1152]{1,0:T(8,128)(2,1)} %bitcast.7), custom_call_target="tpu_custom_call" | custom-call | tf_op jit(solution)/shard_map/project/pallas_call | solution.py:286

commit v3 on v2

v3 whole, which is shorter than its diff:
```python
import functools

import jax
import jax.numpy as jnp
from jax import lax
from jax.experimental import pallas as pl
from jax.experimental.pallas import tpu as pltpu
from jax.sharding import PartitionSpec as P

DH = 32
NEAR = 2
LANES = 128
PER = LANES // DH
CHUNKS = 3

guide_scale = 4.5
epsilon = 1e-06


def head_mask(rows, block):
    row = lax.broadcasted_iota(jnp.int32, (rows, LANES), 0) // DH
    lane = lax.broadcasted_iota(jnp.int32, (rows, LANES), 1) // DH
    return lane == (block if rows == DH else row)


def split_rows(height):
    units = height // 16
    sizes = [(units * (c + 1)) // CHUNKS - (units * c) // CHUNKS for c in range(CHUNKS)]
    return [(16 * sum(sizes[:c]), 16 * sizes[c]) for c in range(CHUNKS)]


def guided_kernel(
    n, bits, ff_ref, q_ref, k_ref, v_ref, w_ref, o_ref,
    kbuf, vbuf, qbuf, wbuf, own_att, comb, obuf, frames, near_out, near_in, tot, pre, tot_out, tot_in, fin, other,
    load_sem, late_sem, out_sem, tot_send, tot_recv, near_send, near_recv, q_sem, fin_sem,
):
    fr = frames.shape[0]
    ft = kbuf.shape[0] // fr
    groups = kbuf.shape[1] // LANES
    base = groups * DH
    chunks = split_rows(frames.shape[1])
    me = lax.axis_index("tm")
    other_core = 1 - lax.axis_index("cfg")

    loads = []
    for f in range(fr):
        rows = pl.ds(f * ft, ft)
        for which, (src, dst) in enumerate(((k_ref, kbuf), (v_ref, vbuf))):
            copy = pltpu.make_async_copy(src.at[rows], dst.at[rows], load_sem.at[2 * f + which])
            copy.start()
            loads.append(copy)

    def partner(k):
        bit = (me // (1 << k)) % 2
        return bit, me + (1 - 2 * bit) * (1 << k)

    barrier = pltpu.get_barrier_semaphore()
    pl.semaphore_signal(barrier, inc=1, device_id={"cfg": other_core})
    count = jnp.int32(1 + bits)
    for k in range(bits):
        pl.semaphore_signal(barrier, inc=1, device_id={"tm": partner(k)[1]})
    for d in range(1, NEAR + 1):
        @pl.when(me + d < n)
        def _():
            pl.semaphore_signal(barrier, inc=1, device_id={"tm": me + d})

        @pl.when(me >= d)
        def _():
            pl.semaphore_signal(barrier, inc=1, device_id={"tm": me - d})

        count = count + jnp.where(me + d < n, 1, 0) + jnp.where(me >= d, 1, 0)

    masks = [head_mask(DH, a) for a in range(PER)]
    for f in range(fr):
        loads[2 * f].wait()
        loads[2 * f + 1].wait()
        frames[f, base:, :] = jnp.zeros((frames.shape[1] - base, LANES), jnp.float32)
        for g in range(groups):
            cols = slice(g * LANES, (g + 1) * LANES)
            keys = jnp.maximum(kbuf[f * ft:(f + 1) * ft, cols], 0)
            values = vbuf[f * ft:(f + 1) * ft, cols]
            full = lax.dot_general(
                values, keys, (((0,), (0,)), ((), ())), preferred_element_type=jnp.float32
            )
            compact = jnp.zeros((DH, LANES), jnp.float32)
            for a in range(PER):
                compact = jnp.where(masks[a], full[a * DH:(a + 1) * DH], compact)
            frames[f, g * DH:(g + 1) * DH, :] = compact
            frames[f, base + g:base + g + 1, :] = jnp.sum(
                keys.astype(jnp.float32), axis=0, keepdims=True
            )
    columns = wbuf.shape[0]
    late = [
        pltpu.make_async_copy(q_ref, qbuf.at[0], late_sem.at[0]),
        pltpu.make_async_copy(
            w_ref.at[pl.ds(pl.multiple_of((1 - other_core) * columns, 16), columns)],
            wbuf, late_sem.at[1],
        ),
    ]
    for copy in late:
        copy.start()
    near_out[...] = frames[...].astype(jnp.bfloat16)
    total = frames[0]
    for f in range(1, fr):
        total = total + frames[f]
    tot[...] = total
    tot_out[0] = total.astype(jnp.bfloat16)
    pre[...] = jnp.zeros_like(pre)
    for d in range(1, NEAR + 1):
        @pl.when(me < d)
        def _():
            near_in[d - 1] = jnp.zeros(near_in.shape[1:], jnp.bfloat16)

    pl.semaphore_wait(barrier, count)

    def near_copy(d):
        return pltpu.make_async_remote_copy(
            src_ref=near_out, dst_ref=near_in.at[d - 1], send_sem=near_send.at[d - 1],
            recv_sem=near_recv.at[d - 1], device_id={"tm": me + d},
        )

    def start_near(d):
        @pl.when(me + d < n)
        def _():
            near_copy(d).start()

    q_copy = pltpu.make_async_remote_copy(
        src_ref=q_ref, dst_ref=qbuf.at[1], send_sem=q_sem.at[0], recv_sem=q_sem.at[1],
        device_id={"cfg": other_core},
    )
    def total_copy(k, c):
        part = pl.ds(*chunks[c])
        return pltpu.make_async_remote_copy(
            src_ref=tot_out.at[k, part], dst_ref=tot_in.at[k, part],
            send_sem=tot_send.at[k, c], recv_sem=tot_recv.at[k, c],
            device_id={"tm": partner(k)[1]},
        )

    def send_total(k, c):
        if k < bits - 1:
            total_copy(k, c).start()
        else:
            @pl.when(partner(k)[0] == 0)
            def _():
                total_copy(k, c).start()

    for c in range(len(chunks)):
        send_total(0, c)
    start_near(2)
    q_copy.start()
    for k in range(bits):
        bit = partner(k)[0]
        for c, (lo, size) in enumerate(chunks):
            part = slice(lo, lo + size)
            if k < bits - 1:
                total_copy(k, c).wait_recv()
                got = tot_in[k, part].astype(jnp.float32)
                pre[part] += jnp.where(bit == 1, 1.0, 0.0) * got
                summed = tot[part] + got
                tot[part] = summed
                tot_out[k + 1, part] = summed.astype(jnp.bfloat16)
                send_total(k + 1, c)
            else:
                @pl.when(bit == 1)
                def _():
                    total_copy(k, c).wait_recv()
                    pre[part] += tot_in[k, part].astype(jnp.float32)
        if k == 0:
            start_near(1)
    for k in range(bits):
        for c in range(len(chunks)):
            if k < bits - 1:
                total_copy(k, c).wait_send()
            else:
                @pl.when(partner(k)[0] == 0)
                def _():
                    total_copy(k, c).wait_send()

    for d in range(1, NEAR + 1):
        @pl.when(me >= d)
        def _():
            near_copy(d).wait_recv()

        @pl.when(me + d < n)
        def _():
            near_copy(d).wait_send()

    for j in range(fr):
        first = ff_ref[j]
        whole = first == 0
        acc = jnp.where(whole, 1.0, 0.0) * pre[...]
        for f in range(j + 1):
            acc = acc + jnp.where(me * fr + f >= first, 1.0, 0.0) * frames[f]
        for d in range(1, NEAR + 1):
            for f in range(fr):
                inside = jnp.logical_and(first > 0, (me - d) * fr + f >= first)
                acc = acc + jnp.where(inside, 1.0, 0.0) * near_in[d - 1, f].astype(jnp.float32)
        fin[j] = acc
    fin_copy = pltpu.make_async_remote_copy(
        src_ref=fin, dst_ref=other, send_sem=fin_sem.at[0], recv_sem=fin_sem.at[1],
        device_id={"cfg": other_core},
    )
    fin_copy.start()

    own_scale = jnp.where(other_core == 1, guide_scale, 1.0 - guide_scale)
    other_scale = 1.0 - own_scale
    diagonal = head_mask(LANES, 0)
    tile = ft if ft % 256 == 0 else 2 * LANES

    def attended(b, source, f, g):
        rows = slice(f * ft, (f + 1) * ft)
        cols = slice(g * LANES, (g + 1) * LANES)
        compact = source[f, g * DH:(g + 1) * DH, :]
        sums = source[f, base + g:base + g + 1, :]
        state = jnp.where(diagonal, jnp.concatenate([compact] * PER, axis=0), 0.0)
        total = jnp.where(diagonal, jnp.broadcast_to(sums, (LANES, LANES)), 0.0)
        both = jnp.concatenate([state, total], axis=0)
        upper = both.astype(jnp.bfloat16)
        lower = (both - upper.astype(jnp.float32)).astype(jnp.bfloat16)
        feats = jnp.maximum(qbuf[b, rows, cols], 0)
        both = lax.dot_general(
            jnp.concatenate([feats, feats], axis=1),
            jnp.concatenate([upper, lower], axis=1),
            (((1,), (1,)), ((), ())), preferred_element_type=jnp.float32,
        )
        return rows, cols, both[:, :LANES] / (both[:, LANES:] + epsilon)

    late[0].wait()
    for f in range(fr):
        for g in range(groups):
            rows, cols, value = attended(0, fin, f, g)
            own_att[rows, cols] = own_scale * value
    fin_copy.wait()
    q_copy.wait()
    for f in range(fr):
        for g in range(groups):
            rows, cols, value = attended(1, other, f, g)
            comb[rows, cols] = (own_att[rows, cols] + other_scale * value).astype(jnp.bfloat16)
    late[1].wait()
    outs = []
    for t in range(comb.shape[0] // tile):
        part = slice(t * tile, (t + 1) * tile)
        obuf[:, part] = lax.dot_general(
            wbuf[...], comb[part, :], (((1,), (1,)), ((), ())),
            preferred_element_type=jnp.float32,
        ).astype(obuf.dtype)
        span = pl.ds(t * tile, tile)
        copy = pltpu.make_async_copy(obuf.at[:, span], o_ref.at[:, span], out_sem.at[t])
        copy.start()
        outs.append(copy)
    for copy in outs:
        copy.wait()


def on_device(n, cores, queries, key_vectors, value_vectors, out_weight, first_frame):
    rows, width = queries.shape[1:]
    fr = first_frame.shape[0]
    bits = n.bit_length() - 1
    groups = width // LANES
    height = groups * DH + 16 * pl.cdiv(groups, 16)
    block = (height, LANES)
    flat = lambda a: a.reshape(rows, width)
    queries = flat(queries)
    f32, bf16 = jnp.float32, jnp.bfloat16
    hbm = pl.BlockSpec(memory_space=pltpu.HBM)
    columns = out_weight.shape[1] // cores
    flipped = pl.pallas_call(
        functools.partial(guided_kernel, n, bits),
        name="guided",
        out_shape=jax.ShapeDtypeStruct((columns, rows), bf16),
        in_specs=[pl.BlockSpec(memory_space=pltpu.SMEM), hbm, hbm, hbm, hbm],
        out_specs=hbm,
        scratch_shapes=[
            pltpu.VMEM((rows, width), bf16),
            pltpu.VMEM((rows, width), bf16),
            pltpu.VMEM((2, rows, width), bf16),
            pltpu.VMEM((columns, width), bf16),
            pltpu.VMEM((rows, width), f32),
            pltpu.VMEM((rows, width), bf16),
            pltpu.VMEM((columns, rows), bf16),
            pltpu.VMEM((fr,) + block, f32),
            pltpu.VMEM((fr,) + block, bf16),
            pltpu.VMEM((NEAR, fr) + block, bf16),
            pltpu.VMEM(block, f32),
            pltpu.VMEM(block, f32),
            pltpu.VMEM((bits,) + block, bf16),
            pltpu.VMEM((bits,) + block, bf16),
            pltpu.VMEM((fr,) + block, f32),
            pltpu.VMEM((fr,) + block, f32),
            pltpu.SemaphoreType.DMA((2 * fr,)),
            pltpu.SemaphoreType.DMA((2,)),
            pltpu.SemaphoreType.DMA((rows // LANES,)),
            pltpu.SemaphoreType.DMA((bits, CHUNKS)),
            pltpu.SemaphoreType.DMA((bits, CHUNKS)),
            pltpu.SemaphoreType.DMA((NEAR,)),
            pltpu.SemaphoreType.DMA((NEAR,)),
            pltpu.SemaphoreType.DMA((2,)),
            pltpu.SemaphoreType.DMA((2,)),
        ],
        compiler_params=pltpu.CompilerParams(
            collective_id=0, has_side_effects=True
        ),
    )(first_frame, queries, flat(key_vectors), flat(value_vectors), out_weight.T)

    return flipped.T


def solution(mesh):
    placed = (P("cfg", "tm", None), P("cfg", "tm", None), P("cfg", "tm", None), P(), P("tm"))
    return jax.shard_map(
        functools.partial(on_device, mesh.shape["tm"], mesh.shape["cfg"]),
        mesh=mesh, in_specs=placed, out_specs=P("tm", "cfg"), check_vma=False,
    )
```

time: 32.4 us -> 29.3 us (0.904)
  Pallas kernels: 32.2 us -> 26.3 us
  local copies, waits for them, and re-layouts: 0 us -> 2.76 us
    pallas_call x2 -> x1, Pallas kernels: 32.2 us -> 26.3 us  [on_device(): pl.pallas_call(functools.partial(guided_kernel, n, bits), name='guided',...]
    unnamed x0 -> x1, local copies, waits for them, and re-layouts: none -> 2.76 us
where the time goes in v3:
time: 29.3 us; the launch traced here: 29.1 us
  Pallas kernels  26.3 us (90%)
  local copies, waits for them, and re-layouts  2.76 us (9%)
    pallas_call x1, Pallas kernels, on_device(): pl.pallas_call(functools.partial(guided_kernel, n, bits), name='guided',...  26.3 us
    unnamed x1, local copies, waits for them, and re-layouts  2.76 us

profile of v3, /device:TPU:0, one launch (start us, length us, event | category | flops | bytes accessed | tf_op | source)
XLA Modules:
  0.0 29.1 jit_solution(13930676131886402689)
XLA Ops:
  0.0 26.3 %guided.1 = bf16[1120,768]{1,0:T(8,128)(2,1)} custom-call(s32[2]{0:T(128)} %ff_ref.1, bf16[768,1152]{1,0:T(8,128)(2,1)} %bitcast.7, bf16[768,1152]{1,0:T(8,128)(2,1)} %bitcast.8, bf16[768,1152]{1,0:T(8,128)(2,1)} %bitcast.9, bf16[2240,1152]{1,0:T(8,128)(2,1)} %bitcast.6), custom_call_target="tpu_custom_call" | custom-call | tf_op jit(solution)/shard_map/guided/pallas_call | solution.py:267
  26.3 2.8 %copy.7 = bf16[768,1120]{0,1:T(8,128)(2,1)} copy(bf16[768,1120]{0,1:T(8,128)(2,1)} %bitcast.5) | data formatting | bytes 3440640
